TPU v7x, 32 devices: a whole 2x2x4 slice. The times are simulated.
32 devices in a mesh: pw: 8 (over y, x, core), mode: 4 (over z).
Axes of the slice: x: 2, y: 2, z: 4, core: 2. Of those that a mesh axis runs over, the one named last changes fastest.
Arguments:
- wave_coeffs: bfloat16 [2, 192, 32768], P(None, 'mode', 'pw'), may hold values from -0.03125 to 0.03125
- sphere_map: int32 [32768], P('pw'), may hold values from 0 to 32768, as said below
- wave_kq: bfloat16 [192, 64, 64, 128], P(None, 'pw'), may hold values from -6 to 6
- potential: bfloat16 [4, 64, 64, 128], P('mode', 'pw'), may hold values from -6 to 6
- shift_map: int32 [3], replicated, may hold values from -1 to 1
Outputs:
- coupling: float32 [192, 2, 192, 4], P('pw', None, None, 'mode')
Inputs may be any that keep to these rules, and one draw needn't show every extreme that they name: `sphere_map`: entries 4096 * p to 4096 * (p + 1) - 1 belong to pw shard p, whose grid planes are g1 = p * 64 / 8 and the next ones. A live entry is a cell of that shard's planes, numbered (local plane * 64 + g2) * 64 + g3, and live entries of one shard are distinct; the value 32768 marks an unused slot. Some shards use all their slots.
All inputs are finite; a program needn't handle non-finite values.
Results may differ from a plain program's by a relative error of at most 0.023.
Values may be sent and summed in bfloat16 or wider, within the bound.
No kernel may reach another device: no remote copies, remote signals or barrier semaphores. Data moves between devices by JAX's collectives and lax.ppermute only.
A program may use at most 256 MiB of HBM per device.

v0:
```python
import math
import jax
import jax.numpy as jnp
from jax import lax
from jax.sharding import PartitionSpec as P

NG = 64


def dft_matrix():
    positions = jnp.arange(NG, dtype=jnp.int32)
    angles = (positions[:, None] * positions[None, :] % NG).astype(jnp.float32) * (
        2.0 * math.pi / NG
    )
    cosine = jnp.cos(angles)
    sine_table = jnp.sin(angles)
    upper = jnp.concatenate([cosine, sine_table], 1)
    lower = jnp.concatenate([-sine_table, cosine], 1)
    return jnp.concatenate([upper, lower], 0).astype(jnp.bfloat16)


def place_cells(coeffs, sphere_map, slab_cells):
    rows = coeffs.shape[0] * coeffs.shape[1]
    flat_coeffs = coeffs.reshape(rows, coeffs.shape[2])
    slot_count = sphere_map.shape[0]
    block = min(1024, slot_count)
    cell_ids = jnp.arange(slab_cells, dtype=jnp.int32)

    def add_block(index, total):
        start = index * block
        targets = lax.dynamic_slice_in_dim(sphere_map, start, block, 0)
        selector = (targets[:, None] == cell_ids[None, :]).astype(jnp.bfloat16)
        values = lax.dynamic_slice_in_dim(flat_coeffs, start, block, 1)
        return total + jnp.dot(values, selector, preferred_element_type=jnp.float32)

    total = lax.fori_loop(
        0, slot_count // block, add_block, jnp.zeros((rows, slab_cells), jnp.float32)
    )
    return total.astype(jnp.bfloat16)


def transform(coeffs, sphere_map, matrix):
    band_count = coeffs.shape[1]
    planes = NG // lax.axis_size("pw")
    slab_cells = planes * NG * NG
    grid_cells = place_cells(coeffs, sphere_map, slab_cells)
    grid_cells = (
        grid_cells.reshape(2, band_count, planes, NG, NG)
        .transpose(1, 2, 3, 0, 4)
        .reshape(band_count, planes, NG, 2 * NG)
    )
    partial_value = jnp.dot(grid_cells, matrix, preferred_element_type=jnp.float32).astype(
        jnp.bfloat16
    )
    partial_value = (
        partial_value.reshape(band_count, planes, NG, 2, NG)
        .transpose(0, 1, 4, 3, 2)
        .reshape(band_count, planes, NG, 2 * NG)
    )
    partial_value = jnp.dot(partial_value, matrix, preferred_element_type=jnp.float32).astype(
        jnp.bfloat16
    )
    partial_value = (
        partial_value.reshape(band_count, planes, NG, 2, NG)
        .transpose(0, 4, 1, 2, 3)
        .reshape(band_count, NG, planes, 2 * NG)
    )
    received = lax.all_to_all(partial_value, "pw", split_axis=1, concat_axis=2, tiled=True)
    row_count = received.shape[0]
    columns = received.shape[1]
    arranged = (
        received.reshape(row_count, columns, NG, NG, 2)
        .transpose(0, 1, 3, 4, 2)
        .reshape(row_count, columns, NG, 2 * NG)
    )
    return jnp.dot(arranged, matrix, preferred_element_type=jnp.float32).astype(jnp.bfloat16)


def on_device(wave_coeffs, sphere_map, wave_kq, potential, shift_map):
    matrix = dft_matrix()
    real_k = transform(wave_coeffs, sphere_map, matrix)
    modes_used = lax.all_gather(potential, "mode", axis=0, tiled=True)
    columns = modes_used.shape[1]
    grid_axis = jnp.arange(NG, dtype=jnp.int32)
    column_ids = lax.axis_index("pw") * columns + jnp.arange(columns, dtype=jnp.int32)
    phase_sum = (
        shift_map[0] * grid_axis[None, None, :]
        + shift_map[1] * column_ids[:, None, None]
        + shift_map[2] * grid_axis[None, :, None]
    ) % NG
    angles = phase_sum.astype(jnp.float32) * (2.0 * math.pi / NG)
    phase_cos = jnp.cos(angles)
    phase_sin = jnp.sin(angles)
    pot_real = modes_used[..., :NG].astype(jnp.float32)
    pot_imag = modes_used[..., NG:].astype(jnp.float32)
    phase_real = pot_real * phase_cos + pot_imag * phase_sin
    phase_imag = pot_imag * phase_cos - pot_real * phase_sin
    k_real = real_k[..., :NG].astype(jnp.float32)
    k_imag = real_k[..., NG:].astype(jnp.float32)
    weight_real = phase_real[:, None] * k_real[None] - phase_imag[:, None] * k_imag[None]
    weight_imag = phase_real[:, None] * k_imag[None] + phase_imag[:, None] * k_real[None]
    modes_here = modes_used.shape[0]
    band_count = real_k.shape[0]
    pair_count = modes_here * band_count
    direct = (
        jnp.concatenate([weight_real, weight_imag], -1).astype(jnp.bfloat16).reshape(pair_count, -1)
    )
    swapped = (
        jnp.concatenate([weight_imag, -weight_real], -1)
        .astype(jnp.bfloat16)
        .reshape(pair_count, -1)
    )
    scale_factor = float(NG) ** (-1.5)
    contract = (((1,), (1,)), ((), ()))
    own_rows = wave_kq.shape[0] // lax.axis_size("pw")
    kq_block = wave_kq.reshape(own_rows * lax.axis_size("pw"), -1)
    g_real = lax.dot_general(kq_block, direct, contract, preferred_element_type=jnp.float32)
    g_imag = lax.dot_general(kq_block, swapped, contract, preferred_element_type=jnp.float32)
    joined = jnp.stack([g_real, g_imag], 1) * scale_factor
    summed = lax.psum_scatter(
        joined.reshape(own_rows * lax.axis_size("pw"), 2, modes_here, band_count)
        .transpose(0, 1, 3, 2)
        .astype(jnp.bfloat16),
        "pw",
        scatter_dimension=0,
        tiled=True,
    ).astype(jnp.float32)
    summed = lax.all_to_all(summed, "mode", split_axis=3, concat_axis=2, tiled=True)
    return summed


def solution(mesh):
    placed = (
        P(None, "mode", "pw"),
        P("pw"),
        P(None, "pw", None, None),
        P("mode", "pw", None, None),
        P(),
    )
    return jax.shard_map(
        on_device,
        mesh=mesh,
        in_specs=placed,
        out_specs=P("pw", None, None, "mode"),
        check_vma=False,
    )
```

profile of v0, /device:TPU:0, one launch (start us, length us, event | category | flops | bytes accessed | tf_op | source)
XLA Modules:
  0.0 780.2 jit_solution(4165691497452577595)
XLA Ops:
  6.5 0.2 negate_convert_fusion.1
  6.7 0.1 fusion.30
  6.8 131.0 %while.14 = (s32[]{:T(128)}, f32[96,32768]{1,0:T(8,128)}, bf16[96,4096]{1,0:T(8,128)(2,1)}, s32[4096]{0:T(1024)}, s32[]{:T(128)}, /*index=5*/s32[]{:T(128)}, s32[]{:T(128)}, s32[]{:T(128)}) while((s32[]{:T(128)}, f32[96,32768]{1,0:T(8,128)}, bf16[96,4096]{1,0:T(8,128)(2,1)}, s32[4096]{0:T(1024)}, s32[]{:T(128)}, ...), condition=%wide.region_1.2_spmd.clone, body=%wide.region_0.1_spmd.clone.sunk | while | flops 6482296832 | bytes 25374868 | solution.py:36
  6.9 0.7 dynamic_slice.21
  7.6 31.3 %fusion.40 = f32[96,32768]{1,0:T(8,128)} fusion(s32[1024]{0:T(1024)S(1)} %dynamic_slice.21, f32[96,32768]{1,0:T(8,128)} %get-tuple-element.175, pred[]{:T(512)S(6)} %compare.10, bf16[96,4096]{1,0:T(8,128)(2,1)} %get-tuple-element.184, s32[]{:T(128)S(6)} %select_n.60), kind=kOutput, calls=%fused_computation.4.clone.1 | convolution fusion | flops 6482296832 | bytes 25366532 | tf_op jit(solution)/shard_map/while/body/eval_jaxpr/dot_general | solution.py:34
  38.9 0.7 dynamic_slice.21
  39.6 32.3 %fusion.40 = f32[96,32768]{1,0:T(8,128)} fusion(s32[1024]{0:T(1024)S(1)} %dynamic_slice.21, f32[96,32768]{1,0:T(8,128)} %get-tuple-element.175, pred[]{:T(512)S(6)} %compare.10, bf16[96,4096]{1,0:T(8,128)(2,1)} %get-tuple-element.184, s32[]{:T(128)S(6)} %select_n.60), kind=kOutput, calls=%fused_computation.4.clone.1 | convolution fusion | flops 6482296832 | bytes 25366532 | tf_op jit(solution)/shard_map/while/body/eval_jaxpr/dot_general | solution.py:34
  71.9 0.7 dynamic_slice.21
  72.6 32.3 %fusion.40 = f32[96,32768]{1,0:T(8,128)} fusion(s32[1024]{0:T(1024)S(1)} %dynamic_slice.21, f32[96,32768]{1,0:T(8,128)} %get-tuple-element.175, pred[]{:T(512)S(6)} %compare.10, bf16[96,4096]{1,0:T(8,128)(2,1)} %get-tuple-element.184, s32[]{:T(128)S(6)} %select_n.60), kind=kOutput, calls=%fused_computation.4.clone.1 | convolution fusion | flops 6482296832 | bytes 25366532 | tf_op jit(solution)/shard_map/while/body/eval_jaxpr/dot_general | solution.py:34
  104.9 0.7 dynamic_slice.21
  105.6 32.3 %fusion.40 = f32[96,32768]{1,0:T(8,128)} fusion(s32[1024]{0:T(1024)S(1)} %dynamic_slice.21, f32[96,32768]{1,0:T(8,128)} %get-tuple-element.175, pred[]{:T(512)S(6)} %compare.10, bf16[96,4096]{1,0:T(8,128)(2,1)} %get-tuple-element.184, s32[]{:T(128)S(6)} %select_n.60), kind=kOutput, calls=%fused_computation.4.clone.1 | convolution fusion | flops 6482296832 | bytes 25366532 | tf_op jit(solution)/shard_map/while/body/eval_jaxpr/dot_general | solution.py:34
  137.9 7.9 %convert_element_type.81 = bf16[96,32768]{1,0:T(8,128)(2,1)} convert(f32[96,32768]{1,0:T(8,128)} %get-tuple-element.99) | non-fusion elementwise | flops 3145728 | bytes 18874368 | tf_op jit(solution)/shard_map/convert_element_type | solution.py:39
  145.8 16.2 %reshape.123 = bf16[2,48,8,64,64]{4,3,2,1,0:T(8,128)(2,1)} reshape(bf16[96,32768]{1,0:T(8,128)(2,1)} %convert_element_type.81) | data formatting | bytes 12582912 | tf_op jit(solution)/shard_map/reshape | solution.py:48
  162.0 23.7 %copy.45 = bf16[48,8,64,2,64]{4,3,2,1,0:T(2,128)(2,1)} copy(bf16[48,8,64,2,64]{4,2,1,0,3:T(8,128)(2,1)} %bitcast.64) | data formatting | bytes 12582912 | tf_op jit(solution)/shard_map/transpose | solution.py:49
  185.7 20.7 %reshape.124 = bf16[48,8,64,128]{3,2,1,0:T(8,128)(2,1)} reshape(bf16[48,8,64,2,64]{4,3,2,1,0:T(2,128)(2,1)} %copy.45) | data formatting | bytes 12582912 | tf_op jit(solution)/shard_map/reshape | solution.py:50
  206.4 7.2 convolution_convert_fusion.2
  213.7 21.6 %reshape.125 = bf16[48,8,64,2,64]{4,3,2,1,0:T(2,128)(2,1)} reshape(bf16[48,8,64,128]{3,2,1,0:T(8,128)(2,1)} %convolution_convert_fusion.2) | data formatting | bytes 12582912 | tf_op jit(solution)/shard_map/reshape | solution.py:56
  235.2 41.2 %copy.46 = bf16[48,8,64,2,64]{4,3,2,1,0:T(2,128)(2,1)} copy(bf16[48,8,64,2,64]{2,3,4,1,0:T(2,128)(2,1)} %bitcast.65) | data formatting | bytes 12582912 | tf_op jit(solution)/shard_map/transpose | solution.py:57
  276.5 20.5 %reshape.126 = bf16[48,8,64,128]{3,2,1,0:T(8,128)(2,1)} reshape(bf16[48,8,64,2,64]{4,3,2,1,0:T(2,128)(2,1)} %copy.46) | data formatting | bytes 12582912 | tf_op jit(solution)/shard_map/reshape | solution.py:58
  297.0 7.2 convolution_convert_fusion.1
  304.2 21.6 %reshape.127 = bf16[48,8,64,2,64]{4,3,2,1,0:T(2,128)(2,1)} reshape(bf16[48,8,64,128]{3,2,1,0:T(8,128)(2,1)} %convolution_convert_fusion.1) | data formatting | bytes 12582912 | tf_op jit(solution)/shard_map/reshape | solution.py:64
  325.8 0.0 copy-start.1
  325.8 0.0 copy-start
  325.8 28.0 %copy.47 = bf16[48,8,64,2,64]{4,1,3,2,0:T(8,128)(2,1)} copy(bf16[48,8,64,2,64]{4,3,2,1,0:T(2,128)(2,1)} %reshape.127) | data formatting | bytes 12582912 | tf_op jit(solution)/shard_map/reshape | solution.py:64
  353.8 17.1 %copy.48 = bf16[48,64,8,128]{3,2,0,1:T(8,128)(2,1)} copy(bf16[48,64,8,128]{1,2,3,0:T(8,128)(2,1)} %bitcast.66) | data formatting | bytes 12582912 | tf_op jit(solution)/shard_map/reshape | solution.py:66
  370.9 5.2 all-to-all-start
  376.1 0.0 all-reduce.3.cloned.1.call-start
  376.2 0.0 copy-done.1
  376.2 0.7 fusion.31
  376.8 0.6 iota_multiply_fusion.1
  377.5 0.6 iota_multiply_fusion
  378.1 0.6 add_multiply_fusion
  378.8 0.0 copy-done
  378.8 17.3 %all_gather.3 = bf16[4,8,64,128]{3,2,1,0:T(8,128)(2,1)S(1)} all-gather(bf16[1,8,64,128]{3,2,1,0:T(8,128)(2,1)S(1)} %copy-done), channel_id=1, replica_groups=mesh['pw'=8,'mode'=4] {'mode'}, dimensions={0}, use_global_device_ids=true | all-gather | bytes 655360 | tf_op jit(solution)/shard_map/all_gather | solution.py:82
  396.1 0.1 broadcast_add_fusion
  396.2 1.1 fusion.22
  397.3 0.4 fusion.14
  397.7 50.2 %all-to-all-done = bf16[48,64,8,128]{3,2,0,1:T(8,128)(2,1)} async-done(((bf16[48,64,8,128]{3,2,0,1:T(8,128)(2,1)}), bf16[48,64,8,128]{3,2,0,1:T(8,128)(2,1)}, u32[]{:S(2)}, u32[]{:S(2)}) %all-to-all-start) | async-done | bytes 6291488 | tf_op jit(solution)/shard_map/all_to_all | solution.py:68
  447.9 29.3 %copy.50 = bf16[48,8,8,8,128]{0,3,2,4,1:T(8,128)(2,1)} copy(bf16[48,8,8,8,128]{4,3,0,1,2:T(8,128)(2,1)} %bitcast.12) | data formatting | bytes 12582912 | tf_op jit(solution)/shard_map/all_to_all | solution.py:68
  477.2 17.4 %copy.60 = bf16[48,8,64,128]{3,2,1,0:T(8,128)(2,1)} copy(bf16[48,8,64,128]{0,3,2,1:T(8,128)(2,1)} %bitcast.63) | data formatting | bytes 12582912 | tf_op jit(solution)/shard_map/reshape | solution.py:74
  494.6 4.6 convolution_convert_fusion
  499.3 9.4 %slice_convert_fusion.1 = (f32[48,8,64,64]{3,2,1,0:T(8,128)}, f32[48,8,64,64]{3,2,1,0:T(8,128)}) fusion(bf16[48,8,64,128]{3,2,1,0:T(8,128)(2,1)S(1)} %convolution_convert_fusion), kind=kLoop, calls=%fused_computation.20 | loop fusion | flops 3145728 | bytes 18874368 | tf_op jit(solution)/shard_map/convert_element_type | solution.py:98
  508.7 32.5 %fusion.7 = (bf16[4,48,8,64,64]{4,3,2,1,0:T(8,128)(2,1)}, bf16[4,48,8,64,64]{4,3,2,1,0:T(8,128)(2,1)}, bf16[4,48,8,64,64]{4,3,2,1,0:T(8,128)(2,1)}) fusion(f32[48,8,64,64]{3,2,1,0:T(8,128)} %get-tuple-element.131, f32[4,8,64,64]{3,2,1,0:T(8,128)S(1)} %get-tuple-element.133, f32[48,8,64,64]{3,2,1,0:T(8,128)} %get-tuple-element.130, ...), kind=kLoop, calls=%fused_computation.10 | loop fusion | flops 62914560 | bytes 51380224 | tf_op jit(solution)/shard_map/convert.2
  541.2 56.0 %pad_maximum_fusion = (bf16[4,48,8,64,128]{4,3,2,1,0:T(8,128)(2,1)}, bf16[4,48,8,64,128]{4,3,2,1,0:T(8,128)(2,1)}) fusion(bf16[4,48,8,64,64]{4,3,2,1,0:T(8,128)(2,1)} %get-tuple-element.126, bf16[4,48,8,64,64]{4,3,2,1,0:T(8,128)(2,1)} %get-tuple-element.125, bf16[4,48,8,64,64]{4,3,2,1,0:T(8,128)(2,1)} %get-tuple-element.127), kind=kLoop, calls=%fused_computation.15 | loop fusion | flops 100663296 | bytes 88080384 | tf_op jit(solution)/shard_map/concatenate | solution.py:106
  597.2 29.8 %convert_element_type.88 = bf16[192,65536]{1,0:T(8,128)(2,1)} reshape(bf16[4,48,8,64,128]{4,3,2,1,0:T(8,128)(2,1)} %get-tuple-element.128) | data formatting | bytes 50331648 | tf_op jit(solution)/shard_map/convert_element_type | solution.py:106
  627.0 23.6 %fusion.10 = f32[192,192]{1,0:T(8,128)S(1)} fusion(bf16[192,65536]{1,0:T(8,128)(2,1)} %convert_element_type.88, bf16[24,8,512,128]{3,2,1,0:T(8,128)(2,1)} %bitcast.69), kind=kOutput, calls=%fused_computation.13 | convolution fusion | flops 4831838208 | bytes 50479104 | tf_op jit(solution)/shard_map/dot_general | solution.py:117
  650.6 0.2 copy.52
  650.8 29.8 %convert_element_type.89 = bf16[192,65536]{1,0:T(8,128)(2,1)} reshape(bf16[4,48,8,64,128]{4,3,2,1,0:T(8,128)(2,1)} %get-tuple-element.129) | data formatting | bytes 50331648 | tf_op jit(solution)/shard_map/convert_element_type | solution.py:110
  680.7 0.0 copy-start.2
  680.7 23.4 %fusion.8 = f32[192,192]{1,0:T(8,128)S(1)} fusion(bf16[192,65536]{1,0:T(8,128)(2,1)} %convert_element_type.89, bf16[24,8,512,128]{3,2,1,0:T(8,128)(2,1)} %bitcast.70), kind=kOutput, calls=%fused_computation.11 | convolution fusion | flops 4831838208 | bytes 50479104 | tf_op jit(solution)/shard_map/dot_general | solution.py:118
  704.1 0.2 copy.53
  704.3 1.0 fusion.17
  705.3 0.0 all-reduce.3.cloned.1.call-update
  705.4 0.0 copy-done.2
  705.4 0.6 dynamic-slice
  706.6 53.4 %all-reduce.3.cloned.1.call-done = bf16[192,2,48,4]{2,3,1,0:T(4,128)(2,1)} async-done(((bf16[192,2,48,4]{2,3,1,0:T(4,128)(2,1)}), bf16[192,2,48,4]{2,3,1,0:T(4,128)(2,1)}) %all-reduce.3.cloned.1.call-update) | async-done | bytes 147472
  760.0 0.8 constant_dynamic-slice_fusion
  760.9 0.1 reshape.135
  761.0 10.0 %all_to_all.33 = f32[4,1,2304]{2,1,0:T(1,128)S(1)} all-to-all(f32[4,1,2304]{2,1,0:T(1,128)S(1)} %reshape.135), channel_id=1, replica_groups=mesh['pw'=8,'mode'=4] {'mode'}, dimensions={0} | all-to-all | bytes 73728 | tf_op jit(solution)/shard_map/all_to_all | solution.py:128
  771.0 0.5 broadcast.132
  771.5 0.7 reduce
  772.3 0.1 reshape.136
  772.4 0.8 reshape.133
  (4 shorter events, 0.1 us)
Async XLA Ops:
  325.8 50.4 %copy-start.1 = (s32[3]{0:T(128)S(1)}, s32[3]{0:T(128)}, u32[]{:S(2)}) copy-start(s32[3]{0:T(128)} %param.11) | copy-start | bytes 40
  325.8 53.0 %copy-start = (bf16[1,8,64,128]{3,2,1,0:T(8,128)(2,1)S(1)}, bf16[1,8,64,128]{3,2,1,0:T(8,128)(2,1)}, u32[]{:S(2)}) copy-start(bf16[1,8,64,128]{3,2,1,0:T(8,128)(2,1)} %param.10) | copy-start | bytes 393220
  370.9 77.0 %all-to-all-start = ((bf16[48,64,8,128]{3,2,0,1:T(8,128)(2,1)}), bf16[48,64,8,128]{3,2,0,1:T(8,128)(2,1)}, u32[]{:S(2)}, u32[]{:S(2)}) async-start(bf16[48,64,8,128]{3,2,0,1:T(8,128)(2,1)} %copy.48), calls=%async_computation | async-start | bytes 12582912 | tf_op jit(solution)/shard_map/all_to_all | solution.py:68
  376.1 383.9 %all-reduce.3.cloned.1.call-start = ((), (), s32[]{:S(2)}) async-start(), calls=%async_computation.2 | async-start | bytes 786432
  680.7 24.7 %copy-start.2 = (u32[32]{0:T(128)S(1)}, u32[32]{0:T(128)}, u32[]{:S(2)}) copy-start(u32[32]{0:T(128)} %constant.70) | copy-start | bytes 388
Sparse Core Ops, SparseCore 0:
  705.5 54.5 all-reduce.2
where the time goes:
time: 794 us; the launch traced here: 780 us
  local copies, waits for them, and re-layouts  324 us (41%)
  matrix products  194 us (24%)
  other arithmetic  111 us (14%)
  waiting for transfers between devices  104 us (13%)
  blocking collectives  27.3 us (3%)
  between operations  14.4 us (2%)
    dot_general x4, matrix products, add_block(): return total + jnp.dot(values, selector, preferred_element_type=jnp.float32)  128 us
    reshape x3, local copies, waits for them, and re-layouts, transform(): partial_value.reshape(band_count, planes, NG, 2, NG)  71.2 us
    concatenate x1, other arithmetic, on_device(): jnp.concatenate([weight_real, weight_imag], -1).astype(jnp.bfloat16)  56 us
    unnamed x2, waiting for transfers between devices  53.4 us
    all_to_all x1, waiting for transfers between devices, transform(): lax.all_to_all(partial_value, 'pw', split_axis=1, concat_axis=2, tiled=True)  50.2 us
    transpose x1, local copies, waits for them, and re-layouts, transform(): partial_value = partial_value.reshape(band_count, planes, NG, 2, NG).tran...  41.2 us
    reshape x2, local copies, waits for them, and re-layouts, transform(): partial_value = partial_value.reshape(band_count, planes, NG, 2, NG).tran...  37.6 us
    another operation x3, other arithmetic  32.8 us
  transfers between devices with their start and end apart: 2, of which 2 were waited for; matrix products, arithmetic and copies ran while one was open for 1% of the time, Pallas kernels for 0%

commit v1 on v0

--- a/solution.py
+++ b/solution.py
@@ -65,7 +65,12 @@
         .transpose(0, 4, 1, 2, 3)
         .reshape(band_count, NG, planes, 2 * NG)
     )
-    received = lax.all_to_all(partial_value, "pw", split_axis=1, concat_axis=2, tiled=True)
+    received = jnp.concatenate(
+        lax.all_to_all(
+            jnp.stack(jnp.split(partial_value, lax.axis_size("pw"), axis=1)), "pw", 0, 0
+        ),
+        axis=2,
+    )
     row_count = received.shape[0]
     columns = received.shape[1]
     arranged = (

time: 794 us -> 954 us (1.20)
  local copies, waits for them, and re-layouts: 324 us -> 481 us
    another operation x0 -> x10, local copies, waits for them, and re-layouts: none -> 165 us  [transform(): jnp.stack(jnp.split(partial_value, lax.axis_size('pw'), axis=1))]
    all_to_all x1 -> x0, local copies, waits for them, and re-layouts: 29.3 us -> none  [transform(): lax.all_to_all(partial_value, 'pw', split_axis=1, concat_axis=2, tiled=True)]
    reshape x0 -> x1, local copies, waits for them, and re-layouts: none -> 28.8 us  [transform(): jnp.concatenate(lax.all_to_all(jnp.stack(jnp.split(partial_value, lax.axi...]
    reshape x2 -> x1, local copies, waits for them, and re-layouts: 37.6 us -> 20.5 us  [transform(): partial_value = partial_value.reshape(band_count, planes, NG, 2, NG).tran...]
    unnamed x10 -> x17, local copies, waits for them, and re-layouts: 1.65 us -> 11.7 us
where the time goes in v1:
time: 954 us; the launch traced here: 938 us
  local copies, waits for them, and re-layouts  481 us (50%)
  matrix products  194 us (20%)
  other arithmetic  112 us (12%)
  waiting for transfers between devices  104 us (11%)
  blocking collectives  27.3 us (3%)
  between operations  14.7 us (2%)
    another operation x10, local copies, waits for them, and re-layouts, transform(): jnp.stack(jnp.split(partial_value, lax.axis_size('pw'), axis=1))  165 us
    dot_general x4, matrix products, add_block(): return total + jnp.dot(values, selector, preferred_element_type=jnp.float32)  128 us
    reshape x3, local copies, waits for them, and re-layouts, transform(): partial_value.reshape(band_count, planes, NG, 2, NG)  71.3 us
    concatenate x1, other arithmetic, on_device(): jnp.concatenate([weight_real, weight_imag], -1).astype(jnp.bfloat16)  56 us
    unnamed x2, waiting for transfers between devices  53.4 us
    all_to_all x1, waiting for transfers between devices, transform(): lax.all_to_all(jnp.stack(jnp.split(partial_value, lax.axis_size('pw'), ax...  50.2 us
    transpose x1, local copies, waits for them, and re-layouts, transform(): partial_value = partial_value.reshape(band_count, planes, NG, 2, NG).tran...  41.2 us
    another operation x3, other arithmetic  33.1 us
  transfers between devices with their start and end apart: 2, of which 2 were waited for; matrix products, arithmetic and copies ran while one was open for 1% of the time, Pallas kernels for 0%

profile of v1, /device:TPU:0, one launch (start us, length us, event | category | flops | bytes accessed | tf_op | source)
XLA Modules:
  0.0 938.5 jit_solution(15454655216247000630)
XLA Ops:
  6.8 131.0 %while.14 = (s32[]{:T(128)}, f32[96,32768]{1,0:T(8,128)}, bf16[96,4096]{1,0:T(8,128)(2,1)}, s32[4096]{0:T(1024)}, s32[]{:T(128)}, /*index=5*/s32[]{:T(128)}, s32[]{:T(128)}, s32[]{:T(128)}) while((s32[]{:T(128)}, f32[96,32768]{1,0:T(8,128)}, bf16[96,4096]{1,0:T(8,128)(2,1)}, s32[4096]{0:T(1024)}, s32[]{:T(128)}, ...), condition=%wide.region_1.2_spmd.clone, body=%wide.region_0.1_spmd.clone.sunk | while | flops 6482296832 | bytes 25374868 | solution.py:36
  6.9 0.7 dynamic_slice.21
  7.6 31.3 %fusion.40 = f32[96,32768]{1,0:T(8,128)} fusion(s32[1024]{0:T(1024)S(1)} %dynamic_slice.21, f32[96,32768]{1,0:T(8,128)} %get-tuple-element.183, pred[]{:T(512)S(6)} %compare.10, bf16[96,4096]{1,0:T(8,128)(2,1)} %get-tuple-element.192, s32[]{:T(128)S(6)} %select_n.60), kind=kOutput, calls=%fused_computation.4.clone.1 | convolution fusion | flops 6482296832 | bytes 25366532 | tf_op jit(solution)/shard_map/while/body/eval_jaxpr/dot_general | solution.py:34
  38.9 0.7 dynamic_slice.21
  39.6 32.3 %fusion.40 = f32[96,32768]{1,0:T(8,128)} fusion(s32[1024]{0:T(1024)S(1)} %dynamic_slice.21, f32[96,32768]{1,0:T(8,128)} %get-tuple-element.183, pred[]{:T(512)S(6)} %compare.10, bf16[96,4096]{1,0:T(8,128)(2,1)} %get-tuple-element.192, s32[]{:T(128)S(6)} %select_n.60), kind=kOutput, calls=%fused_computation.4.clone.1 | convolution fusion | flops 6482296832 | bytes 25366532 | tf_op jit(solution)/shard_map/while/body/eval_jaxpr/dot_general | solution.py:34
  71.9 0.7 dynamic_slice.21
  72.6 32.3 %fusion.40 = f32[96,32768]{1,0:T(8,128)} fusion(s32[1024]{0:T(1024)S(1)} %dynamic_slice.21, f32[96,32768]{1,0:T(8,128)} %get-tuple-element.183, pred[]{:T(512)S(6)} %compare.10, bf16[96,4096]{1,0:T(8,128)(2,1)} %get-tuple-element.192, s32[]{:T(128)S(6)} %select_n.60), kind=kOutput, calls=%fused_computation.4.clone.1 | convolution fusion | flops 6482296832 | bytes 25366532 | tf_op jit(solution)/shard_map/while/body/eval_jaxpr/dot_general | solution.py:34
  104.9 0.7 dynamic_slice.21
  105.6 32.3 %fusion.40 = f32[96,32768]{1,0:T(8,128)} fusion(s32[1024]{0:T(1024)S(1)} %dynamic_slice.21, f32[96,32768]{1,0:T(8,128)} %get-tuple-element.183, pred[]{:T(512)S(6)} %compare.10, bf16[96,4096]{1,0:T(8,128)(2,1)} %get-tuple-element.192, s32[]{:T(128)S(6)} %select_n.60), kind=kOutput, calls=%fused_computation.4.clone.1 | convolution fusion | flops 6482296832 | bytes 25366532 | tf_op jit(solution)/shard_map/while/body/eval_jaxpr/dot_general | solution.py:34
  137.9 7.9 convert_element_type.81
  145.7 16.2 %reshape.122 = bf16[2,48,8,64,64]{4,3,2,1,0:T(8,128)(2,1)} reshape(bf16[96,32768]{1,0:T(8,128)(2,1)} %convert_element_type.81) | data formatting | bytes 12582912 | tf_op jit(solution)/shard_map/reshape | solution.py:48
  162.0 23.7 %copy.48 = bf16[48,8,64,2,64]{4,3,2,1,0:T(2,128)(2,1)} copy(bf16[48,8,64,2,64]{4,2,1,0,3:T(8,128)(2,1)} %bitcast.79) | data formatting | bytes 12582912 | tf_op jit(solution)/shard_map/transpose | solution.py:49
  185.7 20.7 %reshape.123 = bf16[48,8,64,128]{3,2,1,0:T(8,128)(2,1)} reshape(bf16[48,8,64,2,64]{4,3,2,1,0:T(2,128)(2,1)} %copy.48) | data formatting | bytes 12582912 | tf_op jit(solution)/shard_map/reshape | solution.py:50
  206.4 7.2 convolution_convert_fusion.2
  213.7 21.6 %reshape.124 = bf16[48,8,64,2,64]{4,3,2,1,0:T(2,128)(2,1)} reshape(bf16[48,8,64,128]{3,2,1,0:T(8,128)(2,1)} %convolution_convert_fusion.2) | data formatting | bytes 12582912 | tf_op jit(solution)/shard_map/reshape | solution.py:56
  235.2 41.2 %copy.49 = bf16[48,8,64,2,64]{4,3,2,1,0:T(2,128)(2,1)} copy(bf16[48,8,64,2,64]{2,3,4,1,0:T(2,128)(2,1)} %bitcast.80) | data formatting | bytes 12582912 | tf_op jit(solution)/shard_map/transpose | solution.py:57
  276.4 20.5 %reshape.125 = bf16[48,8,64,128]{3,2,1,0:T(8,128)(2,1)} reshape(bf16[48,8,64,2,64]{4,3,2,1,0:T(2,128)(2,1)} %copy.49) | data formatting | bytes 12582912 | tf_op jit(solution)/shard_map/reshape | solution.py:58
  296.9 7.2 convolution_convert_fusion.1
  304.2 21.6 %reshape.126 = bf16[48,8,64,2,64]{4,3,2,1,0:T(2,128)(2,1)} reshape(bf16[48,8,64,128]{3,2,1,0:T(8,128)(2,1)} %convolution_convert_fusion.1) | data formatting | bytes 12582912 | tf_op jit(solution)/shard_map/reshape | solution.py:64
  325.7 28.2 %copy.50 = bf16[48,8,64,2,64]{4,1,3,2,0:T(8,128)(2,1)} copy(bf16[48,8,64,2,64]{4,3,2,1,0:T(2,128)(2,1)} %reshape.126) | data formatting | bytes 12582912 | tf_op jit(solution)/shard_map/reshape | solution.py:64
  353.9 70.3 %slice_bitcast_fusion = (bf16[1,48,8,8,128]{2,3,4,1,0:T(8,128)(2,1)}, bf16[1,48,8,8,128]{2,3,4,1,0:T(8,128)(2,1)}, bf16[1,48,8,8,128]{2,3,4,1,0:T(8,128)(2,1)}, ...) fusion(bf16[48,64,8,128]{1,2,3,0:T(8,128)(2,1)} %bitcast.77), kind=kLoop, calls=%fused_computation.19 | loop fusion | bytes 12582912 | tf_op jit(solution)/shard_map/stack | solution.py:70
  424.2 11.6 %copy.51 = bf16[1,48,8,8,128]{4,3,2,1,0:T(8,128)(2,1)S(1)} copy(bf16[1,48,8,8,128]{2,3,4,1,0:T(8,128)(2,1)} %get-tuple-element.137) | data formatting | bytes 1572864 | tf_op jit(solution)/shard_map/stack | solution.py:70
  435.8 0.9 constant_dynamic-update-slice_fusion.7
  436.7 12.0 %copy.52 = bf16[1,48,8,8,128]{4,3,2,1,0:T(8,128)(2,1)} copy(bf16[1,48,8,8,128]{2,3,4,1,0:T(8,128)(2,1)} %get-tuple-element.136) | data formatting | bytes 1572864 | tf_op jit(solution)/shard_map/stack | solution.py:70
  448.7 12.0 %copy.53 = bf16[1,48,8,8,128]{4,3,2,1,0:T(8,128)(2,1)} copy(bf16[1,48,8,8,128]{2,3,4,1,0:T(8,128)(2,1)} %get-tuple-element.135) | data formatting | bytes 1572864 | tf_op jit(solution)/shard_map/stack | solution.py:70
  460.7 12.0 %copy.54 = bf16[1,48,8,8,128]{4,3,2,1,0:T(8,128)(2,1)} copy(bf16[1,48,8,8,128]{2,3,4,1,0:T(8,128)(2,1)} %get-tuple-element.134) | data formatting | bytes 1572864 | tf_op jit(solution)/shard_map/stack | solution.py:70
  472.7 11.5 %copy.55 = bf16[1,48,8,8,128]{4,3,2,1,0:T(8,128)(2,1)S(1)} copy(bf16[1,48,8,8,128]{2,3,4,1,0:T(8,128)(2,1)} %get-tuple-element.133) | data formatting | bytes 1572864 | tf_op jit(solution)/shard_map/stack | solution.py:70
  484.2 11.7 %copy.56 = bf16[1,48,8,8,128]{4,3,2,1,0:T(8,128)(2,1)S(1)} copy(bf16[1,48,8,8,128]{2,3,4,1,0:T(8,128)(2,1)} %get-tuple-element.132) | data formatting | bytes 1572864 | tf_op jit(solution)/shard_map/stack | solution.py:70
  496.0 11.6 %copy.57 = bf16[1,48,8,8,128]{4,3,2,1,0:T(8,128)(2,1)S(1)} copy(bf16[1,48,8,8,128]{2,3,4,1,0:T(8,128)(2,1)} %get-tuple-element.131) | data formatting | bytes 1572864 | tf_op jit(solution)/shard_map/stack | solution.py:70
  507.5 11.6 %copy.58 = bf16[1,48,8,8,128]{4,3,2,1,0:T(8,128)(2,1)S(1)} copy(bf16[1,48,8,8,128]{2,3,4,1,0:T(8,128)(2,1)} %get-tuple-element.130) | data formatting | bytes 1572864 | tf_op jit(solution)/shard_map/stack | solution.py:70
  519.1 2.1 constant_dynamic-update-slice_fusion.6
  521.3 2.0 constant_dynamic-update-slice_fusion.5
  523.3 2.1 constant_dynamic-update-slice_fusion.4
  525.4 0.9 constant_dynamic-update-slice_fusion.3
  526.3 1.0 constant_dynamic-update-slice_fusion.2
  527.3 1.0 constant_dynamic-update-slice_fusion.1
  528.3 0.9 constant_dynamic-update-slice_fusion
  529.2 5.2 all-to-all-start
  534.4 0.6 fusion.31
  535.1 0.6 iota_multiply_fusion.1
  535.7 0.6 iota_multiply_fusion
  536.4 0.6 add_multiply_fusion
  537.0 17.3 %all_gather.3 = bf16[4,8,64,128]{3,2,1,0:T(8,128)(2,1)S(1)} all-gather(bf16[1,8,64,128]{3,2,1,0:T(8,128)(2,1)S(1)} %copy-done), channel_id=1, replica_groups=mesh['pw'=8,'mode'=4] {'mode'}, dimensions={0}, use_global_device_ids=true | all-gather | bytes 655360 | tf_op jit(solution)/shard_map/all_gather | solution.py:87
  554.4 1.1 fusion.22
  555.5 0.4 fusion.14
  556.0 50.2 %all-to-all-done = bf16[8,48,8,8,128]{4,3,2,1,0:T(8,128)(2,1)} async-done(((bf16[8,48,8,8,128]{4,3,2,1,0:T(8,128)(2,1)}), bf16[8,48,8,8,128]{4,3,2,1,0:T(8,128)(2,1)}, u32[]{:S(2)}, u32[]{:S(2)}) %all-to-all-start) | async-done | bytes 6291488 | tf_op jit(solution)/shard_map/all_to_all | solution.py:69
  606.2 28.8 %copy.59 = bf16[48,8,8,8,128]{0,3,2,4,1:T(8,128)(2,1)} copy(bf16[48,8,8,8,128]{4,3,1,0,2:T(8,128)(2,1)} %bitcast.19) | data formatting | bytes 12582912 | tf_op jit(solution)/shard_map/reshape | solution.py:68
  635.0 17.3 %copy.68 = bf16[48,8,64,128]{3,2,1,0:T(8,128)(2,1)} copy(bf16[48,8,64,128]{0,3,2,1:T(8,128)(2,1)} %bitcast.78) | data formatting | bytes 12582912 | tf_op jit(solution)/shard_map/reshape | solution.py:79
  652.3 4.6 convolution_convert_fusion
  657.0 9.4 %slice_convert_fusion.1 = (f32[48,8,64,64]{3,2,1,0:T(8,128)}, f32[48,8,64,64]{3,2,1,0:T(8,128)}) fusion(bf16[48,8,64,128]{3,2,1,0:T(8,128)(2,1)S(1)} %convolution_convert_fusion), kind=kLoop, calls=%fused_computation.28 | loop fusion | flops 3145728 | bytes 18874368 | tf_op jit(solution)/shard_map/convert_element_type | solution.py:103
  666.4 32.8 %fusion.7 = (bf16[4,48,8,64,64]{4,3,2,1,0:T(8,128)(2,1)}, bf16[4,48,8,64,64]{4,3,2,1,0:T(8,128)(2,1)}, bf16[4,48,8,64,64]{4,3,2,1,0:T(8,128)(2,1)}) fusion(f32[48,8,64,64]{3,2,1,0:T(8,128)} %get-tuple-element.139, f32[4,8,64,64]{3,2,1,0:T(8,128)S(1)} %get-tuple-element.141, f32[48,8,64,64]{3,2,1,0:T(8,128)} %get-tuple-element.138, ...), kind=kLoop, calls=%fused_computation.10 | loop fusion | flops 62914560 | bytes 51380224 | tf_op jit(solution)/shard_map/convert.2
  699.1 56.0 %pad_maximum_fusion = (bf16[4,48,8,64,128]{4,3,2,1,0:T(8,128)(2,1)}, bf16[4,48,8,64,128]{4,3,2,1,0:T(8,128)(2,1)}) fusion(bf16[4,48,8,64,64]{4,3,2,1,0:T(8,128)(2,1)} %get-tuple-element.126, bf16[4,48,8,64,64]{4,3,2,1,0:T(8,128)(2,1)} %get-tuple-element.125, bf16[4,48,8,64,64]{4,3,2,1,0:T(8,128)(2,1)} %get-tuple-element.127), kind=kLoop, calls=%fused_computation.15 | loop fusion | flops 100663296 | bytes 88080384 | tf_op jit(solution)/shard_map/concatenate | solution.py:111
  755.2 29.8 %convert_element_type.88 = bf16[192,65536]{1,0:T(8,128)(2,1)} reshape(bf16[4,48,8,64,128]{4,3,2,1,0:T(8,128)(2,1)} %get-tuple-element.128) | data formatting | bytes 50331648 | tf_op jit(solution)/shard_map/convert_element_type | solution.py:111
  785.0 23.6 %fusion.10 = f32[192,192]{1,0:T(8,128)S(1)} fusion(bf16[192,65536]{1,0:T(8,128)(2,1)} %convert_element_type.88, bf16[24,8,512,128]{3,2,1,0:T(8,128)(2,1)} %bitcast.83), kind=kOutput, calls=%fused_computation.13 | convolution fusion | flops 4831838208 | bytes 50479104 | tf_op jit(solution)/shard_map/dot_general | solution.py:122
  808.8 29.8 %convert_element_type.89 = bf16[192,65536]{1,0:T(8,128)(2,1)} reshape(bf16[4,48,8,64,128]{4,3,2,1,0:T(8,128)(2,1)} %get-tuple-element.129) | data formatting | bytes 50331648 | tf_op jit(solution)/shard_map/convert_element_type | solution.py:115
  838.7 23.4 %fusion.8 = f32[192,192]{1,0:T(8,128)S(1)} fusion(bf16[192,65536]{1,0:T(8,128)(2,1)} %convert_element_type.89, bf16[24,8,512,128]{3,2,1,0:T(8,128)(2,1)} %bitcast.84), kind=kOutput, calls=%fused_computation.11 | convolution fusion | flops 4831838208 | bytes 50479104 | tf_op jit(solution)/shard_map/dot_general | solution.py:123
  862.3 1.0 fusion.17
  863.4 0.6 dynamic-slice
  864.6 53.4 %all-reduce.3.cloned.1.call-done = bf16[192,2,48,4]{2,3,1,0:T(4,128)(2,1)} async-done(((bf16[192,2,48,4]{2,3,1,0:T(4,128)(2,1)}), bf16[192,2,48,4]{2,3,1,0:T(4,128)(2,1)}) %all-reduce.3.cloned.1.call-update) | async-done | bytes 147472
  918.0 0.8 constant_dynamic-slice_fusion
  919.0 10.0 %all_to_all.23 = f32[4,1,2304]{2,1,0:T(1,128)S(1)} all-to-all(f32[4,1,2304]{2,1,0:T(1,128)S(1)} %reshape.134), channel_id=1, replica_groups=mesh['pw'=8,'mode'=4] {'mode'}, dimensions={0} | all-to-all | bytes 73728 | tf_op jit(solution)/shard_map/all_to_all | solution.py:133
  929.0 0.5 broadcast.132
  929.5 0.7 reduce
  930.5 0.8 reshape.132
  (19 shorter events, 1.2 us)
Async XLA Ops:
  519.1 15.3 %copy-start.1 = (s32[3]{0:T(128)S(1)}, s32[3]{0:T(128)}, u32[]{:S(2)}) copy-start(s32[3]{0:T(128)} %param.11) | copy-start | bytes 40
  519.1 17.9 %copy-start = (bf16[1,8,64,128]{3,2,1,0:T(8,128)(2,1)S(1)}, bf16[1,8,64,128]{3,2,1,0:T(8,128)(2,1)}, u32[]{:S(2)}) copy-start(bf16[1,8,64,128]{3,2,1,0:T(8,128)(2,1)} %param.10) | copy-start | bytes 393220
  529.2 77.0 %all-to-all-start = ((bf16[8,48,8,8,128]{4,3,2,1,0:T(8,128)(2,1)}), bf16[8,48,8,8,128]{4,3,2,1,0:T(8,128)(2,1)}, u32[]{:S(2)}, u32[]{:S(2)}) async-start(bf16[8,48,8,8,128]{4,3,2,1,0:T(8,128)(2,1)} %constant_dynamic-update-slice_fusion), calls=%async_computation | async-start | bytes 12582912 | tf_op jit(solution)/shard_map/all_to_all | solution.py:69
  534.4 383.7 %all-reduce.3.cloned.1.call-start = ((), (), s32[]{:S(2)}) async-start(), calls=%async_computation.2 | async-start | bytes 786432
  838.7 24.7 %copy-start.2 = (u32[32]{0:T(128)S(1)}, u32[32]{0:T(128)}, u32[]{:S(2)}) copy-start(u32[32]{0:T(128)} %constant.70) | copy-start | bytes 388
Sparse Core Ops, SparseCore 0:
  863.5 54.5 all-reduce.2
